TPU v7x, 32 devices: a whole 2x2x4 slice. The times are simulated.
32 devices in a mesh: row: 2 (over y), col: 4 (over x, core), rep: 4 (over z).
Axes of the slice: x: 2, y: 2, z: 4, core: 2. Of those that a mesh axis runs over, the one named last changes fastest.
Arguments:
- hidden: bfloat16 [512, 7168], P('rep'), may hold values from -6 to 6
- train_weight: bfloat16 [7168, 16384], P(('rep', 'row'), 'col'), may hold values from -0.0625 to 0.0625
- shard_order: int32 [4, 4, 2], replicated, may hold values from 0 to 1, each once within a row
Outputs:
- served_weight: bfloat16 [7168, 16384], P(None, ('col', 'row'))
- projected: float32 [512, 16384], P('rep', ('col', 'row'))
Inputs may be any that keep to these rules, and one draw needn't show every extreme that they name: Each shard_order[c, k] is a permutation of 0 to 1.
All inputs are finite; a program needn't handle non-finite values.
Results may differ from a plain program's by a relative error of at most 0.001.
Values may be sent and summed in bfloat16 or wider, within the bound.
No kernel may reach another device: no remote copies, remote signals or barrier semaphores. Data moves between devices by JAX's collectives and lax.ppermute only.
A program may use at most 128 MiB of HBM per device.

v0:
```python
from collections import deque

import jax
import jax.numpy as jnp
from jax import lax
from jax.experimental import pallas as pl
from jax.sharding import PartitionSpec as P

CHUNK_BYTES = 1 << 19


def unwritten(shape, dtype):
    return pl.pallas_call(
        lambda out: None,
        out_shape=jax.ShapeDtypeStruct(shape, dtype),
        out_specs=pl.BlockSpec(memory_space=pl.ANY),
    )()


def chunk_count(rows_tile, piece_cols, sub_count):
    chunks = sub_count
    while chunks > 1 and rows_tile * piece_cols * 2 // chunks < CHUNK_BYTES:
        chunks //= 2
    return chunks


def shards(hidden, train_weight, shard_order):
    row_count = lax.axis_size("row")
    rep_count = lax.axis_size("rep")
    row = lax.axis_index("row")
    rep = lax.axis_index("rep")
    col = lax.axis_index("col")
    rows_tile, cols_tile = train_weight.shape
    piece_cols = cols_tile // row_count
    sub_count = shard_order.shape[1]
    sub_cols = piece_cols // sub_count
    chunks = chunk_count(rows_tile, piece_cols, sub_count)
    subs_per = sub_count // chunks
    chunk_cols = sub_cols * subs_per

    def cut(array, starts, sizes):
        return lax.dynamic_slice(array, starts, sizes, allow_negative_indices=False)

    last_pick = None

    def pick(chunk, target):
        nonlocal last_pick
        subs = []
        for sub in range(chunk * subs_per, (chunk + 1) * subs_per):
            block = cut(shard_order, (col, sub, target), (1, 1, 1)).reshape(())
            start = block * piece_cols + sub * sub_cols
            if last_pick is not None:
                start, _ = lax.optimization_barrier((start, last_pick))
            subs.append(cut(train_weight, (0, start), (rows_tile, sub_cols)))
        picked = jnp.concatenate(subs, axis=1) if len(subs) > 1 else subs[0]
        last_pick = lax.optimization_barrier(picked)
        return last_pick

    ring = [(i, (i + 1) % rep_count) for i in range(rep_count)]
    served = unwritten((row_count * rep_count * rows_tile, piece_cols), train_weight.dtype)
    totals = [None] * chunks

    def land(data, sources, chunk, hops):
        nonlocal served
        origin = lax.rem(rep + rep_count - hops, rep_count)
        for block, source in zip(data, sources):
            at = (origin * row_count + source) * rows_tile
            served = lax.dynamic_update_slice(
                served, block, (at, chunk * chunk_cols), allow_negative_indices=False
            )
            features = cut(hidden, (0, at), (hidden.shape[0], rows_tile))
            part = jnp.dot(features, block, preferred_element_type=jnp.float32)
            totals[chunk] = part if totals[chunk] is None else totals[chunk] + part

    def hop(data):
        return [lax.ppermute(block, "rep", ring) for block in data]

    flight = deque()
    owns = []
    for chunk in range(chunks):
        own = [pick(chunk, row)]
        owns.append(own)
        flight.append((hop(own), [row], chunk, 1, "o"))
    shifts = range(1, row_count)
    swaps = []
    for chunk in range(chunks):
        swapped = []
        for shift in shifts:
            block = pick(chunk, lax.rem(row + shift, row_count))
            swapped.append(
                lax.ppermute(block, "row", [(i, (i + shift) % row_count) for i in range(row_count)])
            )
        sources = [lax.rem(row + row_count - shift, row_count) for shift in shifts]
        swaps.append((swapped, sources))
        flight.append((hop(swapped), sources, chunk, 1, "s"))
    for chunk in range(chunks):
        land(owns[chunk], [row], chunk, 0)
    for chunk, (swapped, sources) in enumerate(swaps):
        land(swapped, sources, chunk, 0)
    while flight:
        data, sources, chunk, hops, tag = flight.popleft()
        if hops + 1 < rep_count:
            flight.append((hop(data), sources, chunk, hops + 1, tag))
        land(data, sources, chunk, hops)
    return (served, jnp.concatenate(totals, axis=1))


def solution(mesh):
    placed = (P("rep", None), P(("rep", "row"), "col"), P())

    return jax.shard_map(
        shards,
        mesh=mesh,
        in_specs=placed,
        out_specs=(P(None, ("col", "row")), P("rep", ("col", "row"))),
        check_vma=False,
    )
```

profile of v0, /device:TPU:0, one launch (start us, length us, event | category | flops | bytes accessed | tf_op | source)
XLA Modules:
  0.0 543.4 jit_solution(2331963962726888244)
XLA Ops:
  0.7 1.7 constant_dynamic-slice_fusion.14
  3.0 1.2 constant_dynamic-slice_fusion.8
  4.2 3.1 collective-permute-start.4
  8.0 2.6 constant_dynamic-slice_fusion.7
  11.2 2.6 constant_dynamic-slice_fusion.6
  14.4 2.5 constant_dynamic-slice_fusion.5
  17.6 2.6 constant_dynamic-slice_fusion.3
  20.1 1.6 collective-permute-start
  22.4 2.6 constant_dynamic-slice_fusion.2
  26.1 2.7 constant_dynamic-slice_fusion.1
  28.7 1.6 collective-permute-start.2
  31.0 2.6 constant_dynamic-slice_fusion
  33.9 1.5 fusion.44
  35.4 1.5 fusion.46
  36.9 1.0 constant_dynamic-update-slice_fusion.7
  37.9 2.2 constant_dynamic-update-slice_fusion.31
  40.0 1.5 fusion.48
  41.5 2.2 constant_dynamic-update-slice_fusion.23
  43.7 2.2 constant_dynamic-update-slice_fusion.15
  46.2 1.7 collective-permute-start.5
  47.8 2.2 constant_dynamic-update-slice_fusion.6
  50.0 51.2 %collective-permute-done.3 = bf16[896,512]{1,0:T(8,128)(2,1)} collective-permute-done((bf16[896,512]{1,0:T(8,128)(2,1)}, bf16[896,512]{1,0:T(8,128)(2,1)}, u32[]{:S(2)}, u32[]{:S(2)}) %collective-permute-start.3) | collective-permute-done | bytes 917536 | tf_op jit(solution)/shard_map/ppermute | solution.py:91
  101.2 1.6 collective-permute-start.6
  102.8 1.5 convolution_add_fusion.4
  104.3 1.6 collective-permute-start.7
  106.0 1.5 convolution_add_fusion.9
  107.8 1.5 convolution_add_fusion.14
  109.3 2.2 constant_dynamic-update-slice_fusion.30
  111.5 2.2 constant_dynamic-update-slice_fusion.22
  113.6 2.2 constant_dynamic-update-slice_fusion.14
  115.8 1.5 convolution_add_fusion.19
  117.3 28.8 %collective-permute-done.7 = bf16[896,512]{1,0:T(8,128)(2,1)S(1)} collective-permute-done((bf16[896,512]{1,0:T(8,128)(2,1)}, bf16[896,512]{1,0:T(8,128)(2,1)S(1)}, u32[]{:S(2)}, u32[]{:S(2)}) %collective-permute-start.7) | collective-permute-done | bytes 917536 | tf_op jit(solution)/shard_map/ppermute | solution.py:76
  146.5 1.4 collective-permute-start.10
  148.5 2.2 constant_dynamic-update-slice_fusion.5
  150.7 3.3 collective-permute-start.15
  154.3 1.0 constant_dynamic-update-slice_fusion.29
  155.3 1.5 convolution_add_fusion.18
  156.8 1.0 constant_dynamic-update-slice_fusion.21
  157.8 8.0 %collective-permute-done.8 = bf16[896,512]{1,0:T(8,128)(2,1)S(1)} collective-permute-done((bf16[896,512]{1,0:T(8,128)(2,1)}, bf16[896,512]{1,0:T(8,128)(2,1)S(1)}, u32[]{:S(2)}, u32[]{:S(2)}) %collective-permute-start.8) | collective-permute-done | bytes 917536 | tf_op jit(solution)/shard_map/ppermute | solution.py:76
  165.8 19.7 %collective-permute-done.9 = bf16[896,512]{1,0:T(8,128)(2,1)S(1)} collective-permute-done((bf16[896,512]{1,0:T(8,128)(2,1)}, bf16[896,512]{1,0:T(8,128)(2,1)S(1)}, u32[]{:S(2)}, u32[]{:S(2)}) %collective-permute-start.9) | collective-permute-done | bytes 917536 | tf_op jit(solution)/shard_map/ppermute | solution.py:76
  185.5 1.0 constant_dynamic-update-slice_fusion.13
  188.4 16.7 %collective-permute-done.10 = bf16[896,512]{1,0:T(8,128)(2,1)S(1)} collective-permute-done((bf16[896,512]{1,0:T(8,128)(2,1)}, bf16[896,512]{1,0:T(8,128)(2,1)S(1)}, u32[]{:S(2)}, u32[]{:S(2)}) %collective-permute-start.10) | collective-permute-done | bytes 917536 | tf_op jit(solution)/shard_map/ppermute | solution.py:76
  205.1 1.0 constant_dynamic-update-slice_fusion.20
  206.1 38.3 %collective-permute-done.15 = bf16[896,512]{1,0:T(8,128)(2,1)S(1)} collective-permute-done((bf16[896,512]{1,0:T(8,128)(2,1)S(1)}, bf16[896,512]{1,0:T(8,128)(2,1)S(1)}, u32[]{:S(2)}, u32[]{:S(2)}) %collective-permute-start.15) | collective-permute-done | bytes 917536 | tf_op jit(solution)/shard_map/ppermute | solution.py:76
  244.8 1.4 collective-permute-start.17
  246.5 17.6 %collective-permute-done.11 = bf16[896,512]{1,0:T(8,128)(2,1)S(1)} collective-permute-done((bf16[896,512]{1,0:T(8,128)(2,1)}, bf16[896,512]{1,0:T(8,128)(2,1)S(1)}, u32[]{:S(2)}, u32[]{:S(2)}) %collective-permute-start.11) | collective-permute-done | bytes 917536 | tf_op jit(solution)/shard_map/ppermute | solution.py:76
  264.1 19.7 %collective-permute-done.13 = bf16[896,512]{1,0:T(8,128)(2,1)S(1)} collective-permute-done((bf16[896,512]{1,0:T(8,128)(2,1)S(1)}, bf16[896,512]{1,0:T(8,128)(2,1)S(1)}, u32[]{:S(2)}, u32[]{:S(2)}) %collective-permute-start.13) | collective-permute-done | bytes 917536 | tf_op jit(solution)/shard_map/ppermute | solution.py:76
  284.1 1.0 constant_dynamic-update-slice_fusion.12
  286.0 17.4 %collective-permute-done.12 = bf16[896,512]{1,0:T(8,128)(2,1)S(1)} collective-permute-done((bf16[896,512]{1,0:T(8,128)(2,1)}, bf16[896,512]{1,0:T(8,128)(2,1)S(1)}, u32[]{:S(2)}, u32[]{:S(2)}) %collective-permute-start.12) | collective-permute-done | bytes 917536 | tf_op jit(solution)/shard_map/ppermute | solution.py:76
  303.4 1.0 constant_dynamic-update-slice_fusion.3
  304.7 1.0 constant_dynamic-update-slice_fusion.27
  307.0 16.1 %collective-permute-done.16 = bf16[896,512]{1,0:T(8,128)(2,1)S(1)} collective-permute-done((bf16[896,512]{1,0:T(8,128)(2,1)S(1)}, bf16[896,512]{1,0:T(8,128)(2,1)S(1)}, u32[]{:S(2)}, u32[]{:S(2)}) %collective-permute-start.16) | collective-permute-done | bytes 917536 | tf_op jit(solution)/shard_map/ppermute | solution.py:76
  323.1 1.0 constant_dynamic-update-slice_fusion.11
  324.1 18.7 %collective-permute-done.17 = bf16[896,512]{1,0:T(8,128)(2,1)S(1)} collective-permute-done((bf16[896,512]{1,0:T(8,128)(2,1)S(1)}, bf16[896,512]{1,0:T(8,128)(2,1)S(1)}, u32[]{:S(2)}, u32[]{:S(2)}) %collective-permute-start.17) | collective-permute-done | bytes 917536 | tf_op jit(solution)/shard_map/ppermute | solution.py:76
  342.8 1.0 constant_dynamic-update-slice_fusion.2
  344.7 17.7 %collective-permute-done.18 = bf16[896,512]{1,0:T(8,128)(2,1)S(1)} collective-permute-done((bf16[896,512]{1,0:T(8,128)(2,1)S(1)}, bf16[896,512]{1,0:T(8,128)(2,1)S(1)}, u32[]{:S(2)}, u32[]{:S(2)}) %collective-permute-start.18) | collective-permute-done | bytes 917536 | tf_op jit(solution)/shard_map/ppermute | solution.py:76
  363.4 18.7 %collective-permute-done.19 = bf16[896,512]{1,0:T(8,128)(2,1)S(1)} collective-permute-done((bf16[896,512]{1,0:T(8,128)(2,1)S(1)}, bf16[896,512]{1,0:T(8,128)(2,1)S(1)}, u32[]{:S(2)}, u32[]{:S(2)}) %collective-permute-start.19) | collective-permute-done | bytes 917536 | tf_op jit(solution)/shard_map/ppermute | solution.py:76
  383.1 18.7 %collective-permute-done.23 = bf16[896,512]{1,0:T(8,128)(2,1)S(1)} collective-permute-done((bf16[896,512]{1,0:T(8,128)(2,1)S(1)}, bf16[896,512]{1,0:T(8,128)(2,1)S(1)}, u32[]{:S(2)}, u32[]{:S(2)}) %collective-permute-start.23) | collective-permute-done | bytes 917536 | tf_op jit(solution)/shard_map/ppermute | solution.py:76
  402.1 19.3 %collective-permute-done.22 = bf16[896,512]{1,0:T(8,128)(2,1)S(1)} collective-permute-done((bf16[896,512]{1,0:T(8,128)(2,1)S(1)}, bf16[896,512]{1,0:T(8,128)(2,1)S(1)}, u32[]{:S(2)}, u32[]{:S(2)}) %collective-permute-start.22) | collective-permute-done | bytes 917536 | tf_op jit(solution)/shard_map/ppermute | solution.py:76
  421.7 19.3 %collective-permute-done.21 = bf16[896,512]{1,0:T(8,128)(2,1)S(1)} collective-permute-done((bf16[896,512]{1,0:T(8,128)(2,1)S(1)}, bf16[896,512]{1,0:T(8,128)(2,1)S(1)}, u32[]{:S(2)}, u32[]{:S(2)}) %collective-permute-start.21) | collective-permute-done | bytes 917536 | tf_op jit(solution)/shard_map/ppermute | solution.py:76
  441.4 19.3 %collective-permute-done.20 = bf16[896,512]{1,0:T(8,128)(2,1)S(1)} collective-permute-done((bf16[896,512]{1,0:T(8,128)(2,1)S(1)}, bf16[896,512]{1,0:T(8,128)(2,1)S(1)}, u32[]{:S(2)}, u32[]{:S(2)}) %collective-permute-start.20) | collective-permute-done | bytes 917536 | tf_op jit(solution)/shard_map/ppermute | solution.py:76
  463.3 1.0 constant_dynamic-update-slice_fusion.25
  466.3 70.8 %collective-permute-done.27 = bf16[896,512]{1,0:T(8,128)(2,1)S(1)} collective-permute-done((bf16[896,512]{1,0:T(8,128)(2,1)S(1)}, bf16[896,512]{1,0:T(8,128)(2,1)S(1)}, u32[]{:S(2)}, u32[]{:S(2)}) %collective-permute-start.27) | collective-permute-done | bytes 917536 | tf_op jit(solution)/shard_map/ppermute | solution.py:76
  538.4 1.0 pad_maximum_fusion
  (69 shorter events, 21.7 us)
Async XLA Ops:
  0.6 33.3 %copy-start = (bf16[128,7168]{1,0:T(8,128)(2,1)S(1)}, bf16[128,7168]{1,0:T(8,128)(2,1)}, u32[]{:S(2)}) copy-start(bf16[128,7168]{1,0:T(8,128)(2,1)} %param.3) | copy-start | bytes 5505028
  4.2 144.0 %collective-permute-start.4 = (bf16[896,512]{1,0:T(8,128)(2,1)S(1)}, bf16[896,512]{1,0:T(8,128)(2,1)}, u32[]{:S(2)}, u32[]{:S(2)}) collective-permute-start(bf16[896,512]{1,0:T(8,128)(2,1)S(1)} %constant_dynamic-slice_fusion.8), channel_id=1, source_target_pairs={{0,1},{1,2},{2,3},{3,0},{4,5},{5,6},{6,7},{7,4},{8,9},{9,10},{10,1... | collective-permute-start | bytes 2752520 | tf_op jit(solution)/shard_map/ppermute | solution.py:76
  20.1 26.0 %collective-permute-start = (bf16[896,512]{1,0:T(8,128)(2,1)}, bf16[896,512]{1,0:T(8,128)(2,1)}, u32[]{:S(2)}, u32[]{:S(2)}) collective-permute-start(bf16[896,512]{1,0:T(8,128)(2,1)} %constant_dynamic-slice_fusion.3), channel_id=1, source_target_pairs={{0,16},{16,0},{1,17},{17,1},{2,18},{18,2},{3,19},{19,3},{4,20},{20... | collective-permute-start | bytes 2752520 | tf_op jit(solution)/shard_map/ppermute | solution.py:91
  25.0 82.5 %collective-permute-start.1 = (bf16[896,512]{1,0:T(8,128)(2,1)}, bf16[896,512]{1,0:T(8,128)(2,1)}, u32[]{:S(2)}, u32[]{:S(2)}) collective-permute-start(bf16[896,512]{1,0:T(8,128)(2,1)} %constant_dynamic-slice_fusion.2), channel_id=1, source_target_pairs={{0,16},{16,0},{1,17},{17,1},{2,18},{18,2},{3,19},{19,3},{4,20},{20... | collective-permute-start | bytes 2752520 | tf_op jit(solution)/shard_map/ppermute | solution.py:91
  28.7 75.6 %collective-permute-start.2 = (bf16[896,512]{1,0:T(8,128)(2,1)}, bf16[896,512]{1,0:T(8,128)(2,1)}, u32[]{:S(2)}, u32[]{:S(2)}) collective-permute-start(bf16[896,512]{1,0:T(8,128)(2,1)} %constant_dynamic-slice_fusion.1), channel_id=1, source_target_pairs={{0,16},{16,0},{1,17},{17,1},{2,18},{18,2},{3,19},{19,3},{4,20},{20... | collective-permute-start | bytes 2752520 | tf_op jit(solution)/shard_map/ppermute | solution.py:91
  33.6 67.7 %collective-permute-start.3 = (bf16[896,512]{1,0:T(8,128)(2,1)}, bf16[896,512]{1,0:T(8,128)(2,1)}, u32[]{:S(2)}, u32[]{:S(2)}) collective-permute-start(bf16[896,512]{1,0:T(8,128)(2,1)} %constant_dynamic-slice_fusion), channel_id=1, source_target_pairs={{0,16},{16,0},{1,17},{17,1},{2,18},{18,2},{3,19},{19,3},{4,20},{20... | collective-permute-start | bytes 2752520 | tf_op jit(solution)/shard_map/ppermute | solution.py:91
  46.2 104.5 %collective-permute-start.5 = (bf16[896,512]{1,0:T(8,128)(2,1)}, bf16[896,512]{1,0:T(8,128)(2,1)S(1)}, u32[]{:S(2)}, u32[]{:S(2)}) collective-permute-start(bf16[896,512]{1,0:T(8,128)(2,1)} %constant_dynamic-slice_fusion.7), channel_id=1, source_target_pairs={{0,1},{1,2},{2,3},{3,0},{4,5},{5,6},{6,7},{7,4},{8,9},{9,10},{10,1... | collective-permute-start | bytes 2752520 | tf_op jit(solution)/shard_map/ppermute | solution.py:76
  101.2 45.2 %collective-permute-start.6 = (bf16[896,512]{1,0:T(8,128)(2,1)}, bf16[896,512]{1,0:T(8,128)(2,1)S(1)}, u32[]{:S(2)}, u32[]{:S(2)}) collective-permute-start(bf16[896,512]{1,0:T(8,128)(2,1)} %constant_dynamic-slice_fusion.6), channel_id=1, source_target_pairs={{0,1},{1,2},{2,3},{3,0},{4,5},{5,6},{6,7},{7,4},{8,9},{9,10},{10,1... | collective-permute-start | bytes 2752520 | tf_op jit(solution)/shard_map/ppermute | solution.py:76
  104.3 41.8 %collective-permute-start.7 = (bf16[896,512]{1,0:T(8,128)(2,1)}, bf16[896,512]{1,0:T(8,128)(2,1)S(1)}, u32[]{:S(2)}, u32[]{:S(2)}) collective-permute-start(bf16[896,512]{1,0:T(8,128)(2,1)} %constant_dynamic-slice_fusion.5), channel_id=1, source_target_pairs={{0,1},{1,2},{2,3},{3,0},{4,5},{5,6},{6,7},{7,4},{8,9},{9,10},{10,1... | collective-permute-start | bytes 2752520 | tf_op jit(solution)/shard_map/ppermute | solution.py:76
  107.5 58.3 %collective-permute-start.8 = (bf16[896,512]{1,0:T(8,128)(2,1)}, bf16[896,512]{1,0:T(8,128)(2,1)S(1)}, u32[]{:S(2)}, u32[]{:S(2)}) collective-permute-start(bf16[896,512]{1,0:T(8,128)(2,1)} %collective-permute-done), channel_id=1, source_target_pairs={{0,1},{1,2},{2,3},{3,0},{4,5},{5,6},{6,7},{7,4},{8,9},{9,10},{10,1... | collective-permute-start | bytes 2752520 | tf_op jit(solution)/shard_map/ppermute | solution.py:76
  146.1 39.3 %collective-permute-start.9 = (bf16[896,512]{1,0:T(8,128)(2,1)}, bf16[896,512]{1,0:T(8,128)(2,1)S(1)}, u32[]{:S(2)}, u32[]{:S(2)}) collective-permute-start(bf16[896,512]{1,0:T(8,128)(2,1)} %collective-permute-done.1), channel_id=1, source_target_pairs={{0,1},{1,2},{2,3},{3,0},{4,5},{5,6},{6,7},{7,4},{8,9},{9,10},{10,1... | collective-permute-start | bytes 2752520 | tf_op jit(solution)/shard_map/ppermute | solution.py:76
  146.5 58.6 %collective-permute-start.10 = (bf16[896,512]{1,0:T(8,128)(2,1)}, bf16[896,512]{1,0:T(8,128)(2,1)S(1)}, u32[]{:S(2)}, u32[]{:S(2)}) collective-permute-start(bf16[896,512]{1,0:T(8,128)(2,1)} %collective-permute-done.2), channel_id=1, source_target_pairs={{0,1},{1,2},{2,3},{3,0},{4,5},{5,6},{6,7},{7,4},{8,9},{9,10},{10,1... | collective-permute-start | bytes 2752520 | tf_op jit(solution)/shard_map/ppermute | solution.py:76
  148.2 96.6 %collective-permute-start.14 = (bf16[896,512]{1,0:T(8,128)(2,1)S(1)}, bf16[896,512]{1,0:T(8,128)(2,1)S(1)}, u32[]{:S(2)}, u32[]{:S(2)}) collective-permute-start(bf16[896,512]{1,0:T(8,128)(2,1)S(1)} %collective-permute-done.6), channel_id=1, source_target_pairs={{0,1},{1,2},{2,3},{3,0},{4,5},{5,6},{6,7},{7,4},{8,9},{9,10},{10,1... | collective-permute-start | bytes 2752520 | tf_op jit(solution)/shard_map/ppermute | solution.py:76
  150.7 93.7 %collective-permute-start.15 = (bf16[896,512]{1,0:T(8,128)(2,1)S(1)}, bf16[896,512]{1,0:T(8,128)(2,1)S(1)}, u32[]{:S(2)}, u32[]{:S(2)}) collective-permute-start(bf16[896,512]{1,0:T(8,128)(2,1)S(1)} %collective-permute-done.7), channel_id=1, source_target_pairs={{0,1},{1,2},{2,3},{3,0},{4,5},{5,6},{6,7},{7,4},{8,9},{9,10},{10,1... | collective-permute-start | bytes 2752520 | tf_op jit(solution)/shard_map/ppermute | solution.py:76
  165.8 98.3 %collective-permute-start.11 = (bf16[896,512]{1,0:T(8,128)(2,1)}, bf16[896,512]{1,0:T(8,128)(2,1)S(1)}, u32[]{:S(2)}, u32[]{:S(2)}) collective-permute-start(bf16[896,512]{1,0:T(8,128)(2,1)} %collective-permute-done.3), channel_id=1, source_target_pairs={{0,1},{1,2},{2,3},{3,0},{4,5},{5,6},{6,7},{7,4},{8,9},{9,10},{10,1... | collective-permute-start | bytes 2752520 | tf_op jit(solution)/shard_map/ppermute | solution.py:76
  185.5 98.3 %collective-permute-start.13 = (bf16[896,512]{1,0:T(8,128)(2,1)S(1)}, bf16[896,512]{1,0:T(8,128)(2,1)S(1)}, u32[]{:S(2)}, u32[]{:S(2)}) collective-permute-start(bf16[896,512]{1,0:T(8,128)(2,1)S(1)} %collective-permute-done.5), channel_id=1, source_target_pairs={{0,1},{1,2},{2,3},{3,0},{4,5},{5,6},{6,7},{7,4},{8,9},{9,10},{10,1... | collective-permute-start | bytes 2752520 | tf_op jit(solution)/shard_map/ppermute | solution.py:76
  205.1 98.3 %collective-permute-start.12 = (bf16[896,512]{1,0:T(8,128)(2,1)}, bf16[896,512]{1,0:T(8,128)(2,1)S(1)}, u32[]{:S(2)}, u32[]{:S(2)}) collective-permute-start(bf16[896,512]{1,0:T(8,128)(2,1)} %collective-permute-done.4), channel_id=1, source_target_pairs={{0,1},{1,2},{2,3},{3,0},{4,5},{5,6},{6,7},{7,4},{8,9},{9,10},{10,1... | collective-permute-start | bytes 2752520 | tf_op jit(solution)/shard_map/ppermute | solution.py:76
  244.4 78.6 %collective-permute-start.16 = (bf16[896,512]{1,0:T(8,128)(2,1)S(1)}, bf16[896,512]{1,0:T(8,128)(2,1)S(1)}, u32[]{:S(2)}, u32[]{:S(2)}) collective-permute-start(bf16[896,512]{1,0:T(8,128)(2,1)S(1)} %collective-permute-done.8), channel_id=1, source_target_pairs={{0,1},{1,2},{2,3},{3,0},{4,5},{5,6},{6,7},{7,4},{8,9},{9,10},{10,1... | collective-permute-start | bytes 2752520 | tf_op jit(solution)/shard_map/ppermute | solution.py:76
  244.8 98.0 %collective-permute-start.17 = (bf16[896,512]{1,0:T(8,128)(2,1)S(1)}, bf16[896,512]{1,0:T(8,128)(2,1)S(1)}, u32[]{:S(2)}, u32[]{:S(2)}) collective-permute-start(bf16[896,512]{1,0:T(8,128)(2,1)S(1)} %collective-permute-done.9), channel_id=1, source_target_pairs={{0,1},{1,2},{2,3},{3,0},{4,5},{5,6},{6,7},{7,4},{8,9},{9,10},{10,1... | collective-permute-start | bytes 2752520 | tf_op jit(solution)/shard_map/ppermute | solution.py:76
  264.1 98.3 %collective-permute-start.18 = (bf16[896,512]{1,0:T(8,128)(2,1)S(1)}, bf16[896,512]{1,0:T(8,128)(2,1)S(1)}, u32[]{:S(2)}, u32[]{:S(2)}) collective-permute-start(bf16[896,512]{1,0:T(8,128)(2,1)S(1)} %collective-permute-done.10), channel_id=1, source_target_pairs={{0,1},{1,2},{2,3},{3,0},{4,5},{5,6},{6,7},{7,4},{8,9},{9,10},{10,1... | collective-permute-start | bytes 2752520 | tf_op jit(solution)/shard_map/ppermute | solution.py:76
  283.8 98.3 %collective-permute-start.19 = (bf16[896,512]{1,0:T(8,128)(2,1)S(1)}, bf16[896,512]{1,0:T(8,128)(2,1)S(1)}, u32[]{:S(2)}, u32[]{:S(2)}) collective-permute-start(bf16[896,512]{1,0:T(8,128)(2,1)S(1)} %collective-permute-done.11), channel_id=1, source_target_pairs={{0,1},{1,2},{2,3},{3,0},{4,5},{5,6},{6,7},{7,4},{8,9},{9,10},{10,1... | collective-permute-start | bytes 2752520 | tf_op jit(solution)/shard_map/ppermute | solution.py:76
  303.4 98.3 %collective-permute-start.23 = (bf16[896,512]{1,0:T(8,128)(2,1)S(1)}, bf16[896,512]{1,0:T(8,128)(2,1)S(1)}, u32[]{:S(2)}, u32[]{:S(2)}) collective-permute-start(bf16[896,512]{1,0:T(8,128)(2,1)S(1)} %collective-permute-done.15), channel_id=1, source_target_pairs={{0,1},{1,2},{2,3},{3,0},{4,5},{5,6},{6,7},{7,4},{8,9},{9,10},{10,1... | collective-permute-start | bytes 2752520 | tf_op jit(solution)/shard_map/ppermute | solution.py:76
  323.1 98.3 %collective-permute-start.22 = (bf16[896,512]{1,0:T(8,128)(2,1)S(1)}, bf16[896,512]{1,0:T(8,128)(2,1)S(1)}, u32[]{:S(2)}, u32[]{:S(2)}) collective-permute-start(bf16[896,512]{1,0:T(8,128)(2,1)S(1)} %collective-permute-done.14), channel_id=1, source_target_pairs={{0,1},{1,2},{2,3},{3,0},{4,5},{5,6},{6,7},{7,4},{8,9},{9,10},{10,1... | collective-permute-start | bytes 2752520 | tf_op jit(solution)/shard_map/ppermute | solution.py:76
  342.8 98.3 %collective-permute-start.21 = (bf16[896,512]{1,0:T(8,128)(2,1)S(1)}, bf16[896,512]{1,0:T(8,128)(2,1)S(1)}, u32[]{:S(2)}, u32[]{:S(2)}) collective-permute-start(bf16[896,512]{1,0:T(8,128)(2,1)S(1)} %collective-permute-done.13), channel_id=1, source_target_pairs={{0,1},{1,2},{2,3},{3,0},{4,5},{5,6},{6,7},{7,4},{8,9},{9,10},{10,1... | collective-permute-start | bytes 2752520 | tf_op jit(solution)/shard_map/ppermute | solution.py:76
  362.4 98.3 %collective-permute-start.20 = (bf16[896,512]{1,0:T(8,128)(2,1)S(1)}, bf16[896,512]{1,0:T(8,128)(2,1)S(1)}, u32[]{:S(2)}, u32[]{:S(2)}) collective-permute-start(bf16[896,512]{1,0:T(8,128)(2,1)S(1)} %collective-permute-done.12), channel_id=1, source_target_pairs={{0,1},{1,2},{2,3},{3,0},{4,5},{5,6},{6,7},{7,4},{8,9},{9,10},{10,1... | collective-permute-start | bytes 2752520 | tf_op jit(solution)/shard_map/ppermute | solution.py:76
  382.1 156.0 %collective-permute-start.24 = (bf16[896,512]{1,0:T(8,128)(2,1)S(1)}, bf16[896,512]{1,0:T(8,128)(2,1)S(1)}, u32[]{:S(2)}, u32[]{:S(2)}) collective-permute-start(bf16[896,512]{1,0:T(8,128)(2,1)S(1)} %collective-permute-done.16), channel_id=1, source_target_pairs={{0,1},{1,2},{2,3},{3,0},{4,5},{5,6},{6,7},{7,4},{8,9},{9,10},{10,1... | collective-permute-start | bytes 2752520 | tf_op jit(solution)/shard_map/ppermute | solution.py:76
  401.7 136.0 %collective-permute-start.25 = (bf16[896,512]{1,0:T(8,128)(2,1)S(1)}, bf16[896,512]{1,0:T(8,128)(2,1)S(1)}, u32[]{:S(2)}, u32[]{:S(2)}) collective-permute-start(bf16[896,512]{1,0:T(8,128)(2,1)S(1)} %collective-permute-done.17), channel_id=1, source_target_pairs={{0,1},{1,2},{2,3},{3,0},{4,5},{5,6},{6,7},{7,4},{8,9},{9,10},{10,1... | collective-permute-start | bytes 2752520 | tf_op jit(solution)/shard_map/ppermute | solution.py:76
  421.4 116.0 %collective-permute-start.26 = (bf16[896,512]{1,0:T(8,128)(2,1)S(1)}, bf16[896,512]{1,0:T(8,128)(2,1)S(1)}, u32[]{:S(2)}, u32[]{:S(2)}) collective-permute-start(bf16[896,512]{1,0:T(8,128)(2,1)S(1)} %collective-permute-done.18), channel_id=1, source_target_pairs={{0,1},{1,2},{2,3},{3,0},{4,5},{5,6},{6,7},{7,4},{8,9},{9,10},{10,1... | collective-permute-start | bytes 2752520 | tf_op jit(solution)/shard_map/ppermute | solution.py:76
  441.1 96.0 %collective-permute-start.27 = (bf16[896,512]{1,0:T(8,128)(2,1)S(1)}, bf16[896,512]{1,0:T(8,128)(2,1)S(1)}, u32[]{:S(2)}, u32[]{:S(2)}) collective-permute-start(bf16[896,512]{1,0:T(8,128)(2,1)S(1)} %collective-permute-done.19), channel_id=1, source_target_pairs={{0,1},{1,2},{2,3},{3,0},{4,5},{5,6},{6,7},{7,4},{8,9},{9,10},{10,1... | collective-permute-start | bytes 2752520 | tf_op jit(solution)/shard_map/ppermute | solution.py:76
where the time goes:
time: 545 us; the launch traced here: 543 us
  waiting for transfers between devices  436 us (80%)
  local copies, waits for them, and re-layouts  61.9 us (11%)
  matrix products  19.4 us (4%)
  starting transfers between devices  18.8 us (3%)
  between operations  6.23 us (1%)
    ppermute x24, waiting for transfers between devices, hop(): return [lax.ppermute(block, 'rep', ring) for block in data]  385 us
    ppermute x4, waiting for transfers between devices, shards(): lax.ppermute(block, 'row', [(i, (i + shift) % row_count) for i in range(r...  51.3 us
    dynamic_update_slice x32, local copies, waits for them, and re-layouts, land(): lax.dynamic_update_slice(served, block, (at, chunk * chunk_cols), allow_n...  40.9 us
    dynamic_slice x9, local copies, waits for them, and re-layouts, cut(): return lax.dynamic_slice(array, starts, sizes, allow_negative_indices=False)  21 us
    dot_general x32, matrix products, land(): part = jnp.dot(features, block, preferred_element_type=jnp.float32)  19.4 us
    ppermute x24, starting transfers between devices, hop(): return [lax.ppermute(block, 'rep', ring) for block in data]  14.8 us
  transfers between devices with their start and end apart: 28, of which 18 were waited for; matrix products, arithmetic and copies ran while one was open for 14% of the time, Pallas kernels for 0%

commit v1 on v0

--- a/solution.py
+++ b/solution.py
@@ -42,35 +42,39 @@
         return lax.dynamic_slice(array, starts, sizes, allow_negative_indices=False)
 
     last_pick = None
+    group = col
 
     def pick(chunk, target):
-        nonlocal last_pick
+        nonlocal last_pick, group
         subs = []
         for sub in range(chunk * subs_per, (chunk + 1) * subs_per):
-            block = cut(shard_order, (col, sub, target), (1, 1, 1)).reshape(())
+            block = cut(shard_order, (group, sub, target), (1, 1, 1)).reshape(())
             start = block * piece_cols + sub * sub_cols
             if last_pick is not None:
                 start, _ = lax.optimization_barrier((start, last_pick))
             subs.append(cut(train_weight, (0, start), (rows_tile, sub_cols)))
         picked = jnp.concatenate(subs, axis=1) if len(subs) > 1 else subs[0]
-        last_pick = lax.optimization_barrier(picked)
+        if last_pick is None:
+            group, last_pick = lax.optimization_barrier((col, picked))
+        else:
+            last_pick = lax.optimization_barrier(picked)
         return last_pick
 
     ring = [(i, (i + 1) % rep_count) for i in range(rep_count)]
     served = unwritten((row_count * rep_count * rows_tile, piece_cols), train_weight.dtype)
     totals = [None] * chunks
 
-    def land(data, sources, chunk, hops):
+    def land(data, sources, chunk, hops, place=True, multiply=True):
         nonlocal served
         origin = lax.rem(rep + rep_count - hops, rep_count)
         for block, source in zip(data, sources):
             at = (origin * row_count + source) * rows_tile
-            served = lax.dynamic_update_slice(
-                served, block, (at, chunk * chunk_cols), allow_negative_indices=False
-            )
-            features = cut(hidden, (0, at), (hidden.shape[0], rows_tile))
-            part = jnp.dot(features, block, preferred_element_type=jnp.float32)
-            totals[chunk] = part if totals[chunk] is None else totals[chunk] + part
+            if multiply:
+                features = cut(hidden, (0, at), (hidden.shape[0], rows_tile))
+                part = jnp.dot(features, block, preferred_element_type=jnp.float32)
+                totals[chunk] = part if totals[chunk] is None else totals[chunk] + part
+            if place:
+                served = lax.dynamic_update_slice(served, block, (at, chunk * chunk_cols), allow_negative_indices=False)
 
     def hop(data):
         return [lax.ppermute(block, "rep", ring) for block in data]
@@ -101,8 +105,13 @@
         data, sources, chunk, hops, tag = flight.popleft()
         if hops + 1 < rep_count:
             flight.append((hop(data), sources, chunk, hops + 1, tag))
-        land(data, sources, chunk, hops)
-    return (served, jnp.concatenate(totals, axis=1))
+        land(data, sources, chunk, hops, place=bool(flight))
+    early = totals[:-1] + [jnp.zeros_like(totals[-1])]
+    joined = lax.optimization_barrier(jnp.concatenate(early, axis=1))
+    projected = lax.dynamic_update_slice(joined, totals[-1], (0, (chunks - 1) * chunk_cols))
+    projected, data = lax.optimization_barrier((projected, data))
+    land(data, sources, chunk, hops, multiply=False)
+    return (served, projected)
 
 
 def solution(mesh):

time: 545 us -> 525 us (0.963)
  waiting for transfers between devices: 436 us -> 421 us
    ppermute x4, waiting for transfers between devices: 51.3 us -> 41.9 us  [shards(): lax.ppermute(block, 'row', [(i, (i + shift) % row_count) for i in range(r...]
  transfers between devices with their start and end apart: 28 -> 28, of which waited for: 18 -> 22; matrix products, arithmetic and copies ran while one was open for 14% -> 14% of each run, Pallas kernels for 0% -> 0%
where the time goes in v1:
time: 525 us; the launch traced here: 524 us
  waiting for transfers between devices  421 us (80%)
  local copies, waits for them, and re-layouts  62.6 us (12%)
  matrix products  19.4 us (4%)
  starting transfers between devices  13.7 us (3%)
  between operations  5.28 us (1%)
    ppermute x24, waiting for transfers between devices, hop(): return [lax.ppermute(block, 'rep', ring) for block in data]  380 us
    ppermute x4, waiting for transfers between devices, shards(): lax.ppermute(block, 'row', [(i, (i + shift) % row_count) for i in range(r...  41.9 us
    dynamic_update_slice x32, local copies, waits for them, and re-layouts, land(): lax.dynamic_update_slice(served, block, (at, chunk * chunk_cols), allow_n...  41 us
    dynamic_slice x9, local copies, waits for them, and re-layouts, cut(): return lax.dynamic_slice(array, starts, sizes, allow_negative_indices=False)  21.6 us
    dot_general x32, matrix products, land(): part = jnp.dot(features, block, preferred_element_type=jnp.float32)  19.4 us
  transfers between devices with their start and end apart: 28, of which 22 were waited for; matrix products, arithmetic and copies ran while one was open for 14% of the time, Pallas kernels for 0%

profile of v1, /device:TPU:0, one launch (start us, length us, event | category | flops | bytes accessed | tf_op | source)
XLA Modules:
  0.0 523.8 jit_solution(17880395509320067341)
XLA Ops:
  0.7 1.3 fusion.85
  2.0 1.9 constant_dynamic-slice_fusion.8
  3.9 3.1 collective-permute-start.4
  7.0 1.6 constant_dynamic-slice_fusion.14
  9.2 2.6 constant_dynamic-slice_fusion.7
  11.8 1.6 collective-permute-start.5
  13.9 2.6 constant_dynamic-slice_fusion.6
  17.1 2.5 constant_dynamic-slice_fusion.5
  20.1 2.6 constant_dynamic-slice_fusion.3
  22.7 1.6 collective-permute-start
  25.0 2.7 constant_dynamic-slice_fusion.2
  28.7 2.7 constant_dynamic-slice_fusion.1
  31.3 1.6 collective-permute-start.2
  32.9 1.5 fusion.47
  34.4 1.5 fusion.49
  35.9 1.0 constant_dynamic-update-slice_fusion.7
  36.9 2.2 constant_dynamic-update-slice_fusion.31
  39.7 2.2 constant_dynamic-update-slice_fusion.23
  42.2 2.2 constant_dynamic-update-slice_fusion.15
  44.4 2.6 constant_dynamic-slice_fusion
  46.9 1.5 fusion.45
  48.9 1.5 convolution_add_fusion.19
  50.4 2.2 constant_dynamic-update-slice_fusion.6
  52.5 33.0 %collective-permute-done.2 = bf16[896,512]{1,0:T(8,128)(2,1)} collective-permute-done((bf16[896,512]{1,0:T(8,128)(2,1)}, bf16[896,512]{1,0:T(8,128)(2,1)}, u32[]{:S(2)}, u32[]{:S(2)}) %collective-permute-start.2) | collective-permute-done | bytes 917536 | tf_op jit(solution)/shard_map/ppermute | solution.py:95
  85.6 1.6 collective-permute-start.6
  87.2 1.5 convolution_add_fusion.9
  88.7 1.5 convolution_add_fusion.14
  90.2 2.2 constant_dynamic-update-slice_fusion.30
  92.4 2.2 constant_dynamic-update-slice_fusion.22
  94.6 8.9 %collective-permute-done.3 = bf16[896,512]{1,0:T(8,128)(2,1)S(1)} collective-permute-done((bf16[896,512]{1,0:T(8,128)(2,1)}, bf16[896,512]{1,0:T(8,128)(2,1)S(1)}, u32[]{:S(2)}, u32[]{:S(2)}) %collective-permute-start.3) | collective-permute-done | bytes 917536 | tf_op jit(solution)/shard_map/ppermute | solution.py:95
  103.4 1.6 collective-permute-start.8
  106.3 4.5 collective-permute-done.6
  111.2 1.5 convolution_add_fusion.13
  112.7 1.6 collective-permute-start.11
  114.3 1.5 convolution_add_fusion.18
  115.8 2.2 constant_dynamic-update-slice_fusion.5
  118.0 2.2 constant_dynamic-update-slice_fusion.29
  121.1 9.3 %collective-permute-done.7 = bf16[896,512]{1,0:T(8,128)(2,1)S(1)} collective-permute-done((bf16[896,512]{1,0:T(8,128)(2,1)}, bf16[896,512]{1,0:T(8,128)(2,1)S(1)}, u32[]{:S(2)}, u32[]{:S(2)}) %collective-permute-start.7) | collective-permute-done | bytes 917536 | tf_op jit(solution)/shard_map/ppermute | solution.py:80
  130.8 19.3 %collective-permute-done.8 = bf16[896,512]{1,0:T(8,128)(2,1)S(1)} collective-permute-done((bf16[896,512]{1,0:T(8,128)(2,1)}, bf16[896,512]{1,0:T(8,128)(2,1)S(1)}, u32[]{:S(2)}, u32[]{:S(2)}) %collective-permute-start.8) | collective-permute-done | bytes 917536 | tf_op jit(solution)/shard_map/ppermute | solution.py:80
  152.1 17.7 %collective-permute-done.9 = bf16[896,512]{1,0:T(8,128)(2,1)S(1)} collective-permute-done((bf16[896,512]{1,0:T(8,128)(2,1)}, bf16[896,512]{1,0:T(8,128)(2,1)S(1)}, u32[]{:S(2)}, u32[]{:S(2)}) %collective-permute-start.9) | collective-permute-done | bytes 917536 | tf_op jit(solution)/shard_map/ppermute | solution.py:80
  170.8 18.7 %collective-permute-done.10 = bf16[896,512]{1,0:T(8,128)(2,1)S(1)} collective-permute-done((bf16[896,512]{1,0:T(8,128)(2,1)}, bf16[896,512]{1,0:T(8,128)(2,1)S(1)}, u32[]{:S(2)}, u32[]{:S(2)}) %collective-permute-start.10) | collective-permute-done | bytes 917536 | tf_op jit(solution)/shard_map/ppermute | solution.py:80
  189.5 1.0 constant_dynamic-update-slice_fusion.20
  190.4 18.7 %collective-permute-done.11 = bf16[896,512]{1,0:T(8,128)(2,1)S(1)} collective-permute-done((bf16[896,512]{1,0:T(8,128)(2,1)S(1)}, bf16[896,512]{1,0:T(8,128)(2,1)S(1)}, u32[]{:S(2)}, u32[]{:S(2)}) %collective-permute-start.11) | collective-permute-done | bytes 917536 | tf_op jit(solution)/shard_map/ppermute | solution.py:80
  209.1 1.0 constant_dynamic-update-slice_fusion.12
  210.1 18.7 %collective-permute-done.14 = bf16[896,512]{1,0:T(8,128)(2,1)S(1)} collective-permute-done((bf16[896,512]{1,0:T(8,128)(2,1)S(1)}, bf16[896,512]{1,0:T(8,128)(2,1)S(1)}, u32[]{:S(2)}, u32[]{:S(2)}) %collective-permute-start.14) | collective-permute-done | bytes 917536 | tf_op jit(solution)/shard_map/ppermute | solution.py:80
  229.1 19.3 %collective-permute-done.13 = bf16[896,512]{1,0:T(8,128)(2,1)S(1)} collective-permute-done((bf16[896,512]{1,0:T(8,128)(2,1)}, bf16[896,512]{1,0:T(8,128)(2,1)S(1)}, u32[]{:S(2)}, u32[]{:S(2)}) %collective-permute-start.13) | collective-permute-done | bytes 917536 | tf_op jit(solution)/shard_map/ppermute | solution.py:80
  249.1 19.0 %collective-permute-done.12 = bf16[896,512]{1,0:T(8,128)(2,1)S(1)} collective-permute-done((bf16[896,512]{1,0:T(8,128)(2,1)}, bf16[896,512]{1,0:T(8,128)(2,1)S(1)}, u32[]{:S(2)}, u32[]{:S(2)}) %collective-permute-start.12) | collective-permute-done | bytes 917536 | tf_op jit(solution)/shard_map/ppermute | solution.py:80
  269.1 1.0 constant_dynamic-update-slice_fusion.3
  270.1 17.7 %collective-permute-done.15 = bf16[896,512]{1,0:T(8,128)(2,1)S(1)} collective-permute-done((bf16[896,512]{1,0:T(8,128)(2,1)S(1)}, bf16[896,512]{1,0:T(8,128)(2,1)S(1)}, u32[]{:S(2)}, u32[]{:S(2)}) %collective-permute-start.15) | collective-permute-done | bytes 917536 | tf_op jit(solution)/shard_map/ppermute | solution.py:80
  288.1 1.0 constant_dynamic-update-slice_fusion.27
  290.4 17.1 %collective-permute-done.16 = bf16[896,512]{1,0:T(8,128)(2,1)S(1)} collective-permute-done((bf16[896,512]{1,0:T(8,128)(2,1)S(1)}, bf16[896,512]{1,0:T(8,128)(2,1)S(1)}, u32[]{:S(2)}, u32[]{:S(2)}) %collective-permute-start.16) | collective-permute-done | bytes 917536 | tf_op jit(solution)/shard_map/ppermute | solution.py:80
  308.4 18.7 %collective-permute-done.17 = bf16[896,512]{1,0:T(8,128)(2,1)S(1)} collective-permute-done((bf16[896,512]{1,0:T(8,128)(2,1)S(1)}, bf16[896,512]{1,0:T(8,128)(2,1)S(1)}, u32[]{:S(2)}, u32[]{:S(2)}) %collective-permute-start.17) | collective-permute-done | bytes 917536 | tf_op jit(solution)/shard_map/ppermute | solution.py:80
  329.1 17.7 %collective-permute-done.18 = bf16[896,512]{1,0:T(8,128)(2,1)S(1)} collective-permute-done((bf16[896,512]{1,0:T(8,128)(2,1)S(1)}, bf16[896,512]{1,0:T(8,128)(2,1)S(1)}, u32[]{:S(2)}, u32[]{:S(2)}) %collective-permute-start.18) | collective-permute-done | bytes 917536 | tf_op jit(solution)/shard_map/ppermute | solution.py:80
  347.7 18.7 %collective-permute-done.19 = bf16[896,512]{1,0:T(8,128)(2,1)S(1)} collective-permute-done((bf16[896,512]{1,0:T(8,128)(2,1)S(1)}, bf16[896,512]{1,0:T(8,128)(2,1)S(1)}, u32[]{:S(2)}, u32[]{:S(2)}) %collective-permute-start.19) | collective-permute-done | bytes 917536 | tf_op jit(solution)/shard_map/ppermute | solution.py:80
  367.4 18.7 %collective-permute-done.22 = bf16[896,512]{1,0:T(8,128)(2,1)S(1)} collective-permute-done((bf16[896,512]{1,0:T(8,128)(2,1)S(1)}, bf16[896,512]{1,0:T(8,128)(2,1)S(1)}, u32[]{:S(2)}, u32[]{:S(2)}) %collective-permute-start.22) | collective-permute-done | bytes 917536 | tf_op jit(solution)/shard_map/ppermute | solution.py:80
  386.4 19.3 %collective-permute-done.21 = bf16[896,512]{1,0:T(8,128)(2,1)S(1)} collective-permute-done((bf16[896,512]{1,0:T(8,128)(2,1)S(1)}, bf16[896,512]{1,0:T(8,128)(2,1)S(1)}, u32[]{:S(2)}, u32[]{:S(2)}) %collective-permute-start.21) | collective-permute-done | bytes 917536 | tf_op jit(solution)/shard_map/ppermute | solution.py:80
  406.1 19.3 %collective-permute-done.20 = bf16[896,512]{1,0:T(8,128)(2,1)S(1)} collective-permute-done((bf16[896,512]{1,0:T(8,128)(2,1)S(1)}, bf16[896,512]{1,0:T(8,128)(2,1)S(1)}, u32[]{:S(2)}, u32[]{:S(2)}) %collective-permute-start.20) | collective-permute-done | bytes 917536 | tf_op jit(solution)/shard_map/ppermute | solution.py:80
  426.0 1.0 constant_dynamic-update-slice_fusion.1
  427.7 1.0 constant_dynamic-update-slice_fusion.25
  429.7 15.4 %collective-permute-done.23 = bf16[896,512]{1,0:T(8,128)(2,1)S(1)} collective-permute-done((bf16[896,512]{1,0:T(8,128)(2,1)S(1)}, bf16[896,512]{1,0:T(8,128)(2,1)S(1)}, u32[]{:S(2)}, u32[]{:S(2)}) %collective-permute-start.23) | collective-permute-done | bytes 917536 | tf_op jit(solution)/shard_map/ppermute | solution.py:80
  445.4 1.0 constant_dynamic-update-slice_fusion.9
  446.7 57.4 %collective-permute-done.26 = bf16[896,512]{1,0:T(8,128)(2,1)S(1)} collective-permute-done((bf16[896,512]{1,0:T(8,128)(2,1)S(1)}, bf16[896,512]{1,0:T(8,128)(2,1)S(1)}, u32[]{:S(2)}, u32[]{:S(2)}) %collective-permute-start.26) | collective-permute-done | bytes 917536 | tf_op jit(solution)/shard_map/ppermute | solution.py:80
  505.1 14.3 %collective-permute-done.27 = bf16[896,512]{1,0:T(8,128)(2,1)S(1)} collective-permute-done((bf16[896,512]{1,0:T(8,128)(2,1)S(1)}, bf16[896,512]{1,0:T(8,128)(2,1)S(1)}, u32[]{:S(2)}, u32[]{:S(2)}) %collective-permute-start.27) | collective-permute-done | bytes 917536 | tf_op jit(solution)/shard_map/ppermute | solution.py:80
  519.8 1.1 constant_dynamic-update-slice_fusion
  (74 shorter events, 23.4 us)
Async XLA Ops:
  0.6 32.3 %copy-start = (bf16[128,7168]{1,0:T(8,128)(2,1)S(1)}, bf16[128,7168]{1,0:T(8,128)(2,1)}, u32[]{:S(2)}) copy-start(bf16[128,7168]{1,0:T(8,128)(2,1)} %param.3) | copy-start | bytes 5505028
  3.9 108.8 %collective-permute-start.4 = (bf16[896,512]{1,0:T(8,128)(2,1)S(1)}, bf16[896,512]{1,0:T(8,128)(2,1)}, u32[]{:S(2)}, u32[]{:S(2)}) collective-permute-start(bf16[896,512]{1,0:T(8,128)(2,1)S(1)} %constant_dynamic-slice_fusion.8), channel_id=1, source_target_pairs={{0,1},{1,2},{2,3},{3,0},{4,5},{5,6},{6,7},{7,4},{8,9},{9,10},{10,1... | collective-permute-start | bytes 2752520 | tf_op jit(solution)/shard_map/ppermute | solution.py:80
  11.8 99.4 %collective-permute-start.5 = (bf16[896,512]{1,0:T(8,128)(2,1)}, bf16[896,512]{1,0:T(8,128)(2,1)}, u32[]{:S(2)}, u32[]{:S(2)}) collective-permute-start(bf16[896,512]{1,0:T(8,128)(2,1)} %constant_dynamic-slice_fusion.7), channel_id=1, source_target_pairs={{0,1},{1,2},{2,3},{3,0},{4,5},{5,6},{6,7},{7,4},{8,9},{9,10},{10,1... | collective-permute-start | bytes 2752520 | tf_op jit(solution)/shard_map/ppermute | solution.py:80
  22.7 25.7 %collective-permute-start = (bf16[896,512]{1,0:T(8,128)(2,1)}, bf16[896,512]{1,0:T(8,128)(2,1)}, u32[]{:S(2)}, u32[]{:S(2)}) collective-permute-start(bf16[896,512]{1,0:T(8,128)(2,1)} %constant_dynamic-slice_fusion.3), channel_id=1, source_target_pairs={{0,16},{16,0},{1,17},{17,1},{2,18},{18,2},{3,19},{19,3},{4,20},{20... | collective-permute-start | bytes 2752520 | tf_op jit(solution)/shard_map/ppermute | solution.py:95
  27.6 61.0 %collective-permute-start.1 = (bf16[896,512]{1,0:T(8,128)(2,1)}, bf16[896,512]{1,0:T(8,128)(2,1)}, u32[]{:S(2)}, u32[]{:S(2)}) collective-permute-start(bf16[896,512]{1,0:T(8,128)(2,1)} %constant_dynamic-slice_fusion.2), channel_id=1, source_target_pairs={{0,16},{16,0},{1,17},{17,1},{2,18},{18,2},{3,19},{19,3},{4,20},{20... | collective-permute-start | bytes 2752520 | tf_op jit(solution)/shard_map/ppermute | solution.py:95
  31.3 54.3 %collective-permute-start.2 = (bf16[896,512]{1,0:T(8,128)(2,1)}, bf16[896,512]{1,0:T(8,128)(2,1)}, u32[]{:S(2)}, u32[]{:S(2)}) collective-permute-start(bf16[896,512]{1,0:T(8,128)(2,1)} %constant_dynamic-slice_fusion.1), channel_id=1, source_target_pairs={{0,16},{16,0},{1,17},{17,1},{2,18},{18,2},{3,19},{19,3},{4,20},{20... | collective-permute-start | bytes 2752520 | tf_op jit(solution)/shard_map/ppermute | solution.py:95
  48.4 55.0 %collective-permute-start.3 = (bf16[896,512]{1,0:T(8,128)(2,1)}, bf16[896,512]{1,0:T(8,128)(2,1)S(1)}, u32[]{:S(2)}, u32[]{:S(2)}) collective-permute-start(bf16[896,512]{1,0:T(8,128)(2,1)} %constant_dynamic-slice_fusion), channel_id=1, source_target_pairs={{0,16},{16,0},{1,17},{17,1},{2,18},{18,2},{3,19},{19,3},{4,20},{20... | collective-permute-start | bytes 2752520 | tf_op jit(solution)/shard_map/ppermute | solution.py:95
  85.6 25.2 %collective-permute-start.6 = (bf16[896,512]{1,0:T(8,128)(2,1)}, bf16[896,512]{1,0:T(8,128)(2,1)S(1)}, u32[]{:S(2)}, u32[]{:S(2)}) collective-permute-start(bf16[896,512]{1,0:T(8,128)(2,1)} %constant_dynamic-slice_fusion.6), channel_id=1, source_target_pairs={{0,1},{1,2},{2,3},{3,0},{4,5},{5,6},{6,7},{7,4},{8,9},{9,10},{10,1... | collective-permute-start | bytes 2752520 | tf_op jit(solution)/shard_map/ppermute | solution.py:80
  88.7 41.8 %collective-permute-start.7 = (bf16[896,512]{1,0:T(8,128)(2,1)}, bf16[896,512]{1,0:T(8,128)(2,1)S(1)}, u32[]{:S(2)}, u32[]{:S(2)}) collective-permute-start(bf16[896,512]{1,0:T(8,128)(2,1)} %constant_dynamic-slice_fusion.5), channel_id=1, source_target_pairs={{0,1},{1,2},{2,3},{3,0},{4,5},{5,6},{6,7},{7,4},{8,9},{9,10},{10,1... | collective-permute-start | bytes 2752520 | tf_op jit(solution)/shard_map/ppermute | solution.py:80
  103.4 46.7 %collective-permute-start.8 = (bf16[896,512]{1,0:T(8,128)(2,1)}, bf16[896,512]{1,0:T(8,128)(2,1)S(1)}, u32[]{:S(2)}, u32[]{:S(2)}) collective-permute-start(bf16[896,512]{1,0:T(8,128)(2,1)} %collective-permute-done), channel_id=1, source_target_pairs={{0,1},{1,2},{2,3},{3,0},{4,5},{5,6},{6,7},{7,4},{8,9},{9,10},{10,1... | collective-permute-start | bytes 2752520 | tf_op jit(solution)/shard_map/ppermute | solution.py:80
  110.8 59.0 %collective-permute-start.9 = (bf16[896,512]{1,0:T(8,128)(2,1)}, bf16[896,512]{1,0:T(8,128)(2,1)S(1)}, u32[]{:S(2)}, u32[]{:S(2)}) collective-permute-start(bf16[896,512]{1,0:T(8,128)(2,1)} %collective-permute-done.1), channel_id=1, source_target_pairs={{0,1},{1,2},{2,3},{3,0},{4,5},{5,6},{6,7},{7,4},{8,9},{9,10},{10,1... | collective-permute-start | bytes 2752520 | tf_op jit(solution)/shard_map/ppermute | solution.py:80
  111.1 78.3 %collective-permute-start.10 = (bf16[896,512]{1,0:T(8,128)(2,1)}, bf16[896,512]{1,0:T(8,128)(2,1)S(1)}, u32[]{:S(2)}, u32[]{:S(2)}) collective-permute-start(bf16[896,512]{1,0:T(8,128)(2,1)} %collective-permute-done.2), channel_id=1, source_target_pairs={{0,1},{1,2},{2,3},{3,0},{4,5},{5,6},{6,7},{7,4},{8,9},{9,10},{10,1... | collective-permute-start | bytes 2752520 | tf_op jit(solution)/shard_map/ppermute | solution.py:80
  112.7 96.4 %collective-permute-start.11 = (bf16[896,512]{1,0:T(8,128)(2,1)S(1)}, bf16[896,512]{1,0:T(8,128)(2,1)S(1)}, u32[]{:S(2)}, u32[]{:S(2)}) collective-permute-start(bf16[896,512]{1,0:T(8,128)(2,1)S(1)} %collective-permute-done.3), channel_id=1, source_target_pairs={{0,1},{1,2},{2,3},{3,0},{4,5},{5,6},{6,7},{7,4},{8,9},{9,10},{10,1... | collective-permute-start | bytes 2752520 | tf_op jit(solution)/shard_map/ppermute | solution.py:80
  130.5 98.3 %collective-permute-start.14 = (bf16[896,512]{1,0:T(8,128)(2,1)S(1)}, bf16[896,512]{1,0:T(8,128)(2,1)S(1)}, u32[]{:S(2)}, u32[]{:S(2)}) collective-permute-start(bf16[896,512]{1,0:T(8,128)(2,1)S(1)} %collective-permute-done.6), channel_id=1, source_target_pairs={{0,1},{1,2},{2,3},{3,0},{4,5},{5,6},{6,7},{7,4},{8,9},{9,10},{10,1... | collective-permute-start | bytes 2752520 | tf_op jit(solution)/shard_map/ppermute | solution.py:80
  150.1 98.3 %collective-permute-start.13 = (bf16[896,512]{1,0:T(8,128)(2,1)}, bf16[896,512]{1,0:T(8,128)(2,1)S(1)}, u32[]{:S(2)}, u32[]{:S(2)}) collective-permute-start(bf16[896,512]{1,0:T(8,128)(2,1)} %collective-permute-done.5), channel_id=1, source_target_pairs={{0,1},{1,2},{2,3},{3,0},{4,5},{5,6},{6,7},{7,4},{8,9},{9,10},{10,1... | collective-permute-start | bytes 2752520 | tf_op jit(solution)/shard_map/ppermute | solution.py:80
  169.8 98.3 %collective-permute-start.12 = (bf16[896,512]{1,0:T(8,128)(2,1)}, bf16[896,512]{1,0:T(8,128)(2,1)S(1)}, u32[]{:S(2)}, u32[]{:S(2)}) collective-permute-start(bf16[896,512]{1,0:T(8,128)(2,1)} %collective-permute-done.4), channel_id=1, source_target_pairs={{0,1},{1,2},{2,3},{3,0},{4,5},{5,6},{6,7},{7,4},{8,9},{9,10},{10,1... | collective-permute-start | bytes 2752520 | tf_op jit(solution)/shard_map/ppermute | solution.py:80
  189.5 98.3 %collective-permute-start.15 = (bf16[896,512]{1,0:T(8,128)(2,1)S(1)}, bf16[896,512]{1,0:T(8,128)(2,1)S(1)}, u32[]{:S(2)}, u32[]{:S(2)}) collective-permute-start(bf16[896,512]{1,0:T(8,128)(2,1)S(1)} %collective-permute-done.7), channel_id=1, source_target_pairs={{0,1},{1,2},{2,3},{3,0},{4,5},{5,6},{6,7},{7,4},{8,9},{9,10},{10,1... | collective-permute-start | bytes 2752520 | tf_op jit(solution)/shard_map/ppermute | solution.py:80
  209.1 98.3 %collective-permute-start.16 = (bf16[896,512]{1,0:T(8,128)(2,1)S(1)}, bf16[896,512]{1,0:T(8,128)(2,1)S(1)}, u32[]{:S(2)}, u32[]{:S(2)}) collective-permute-start(bf16[896,512]{1,0:T(8,128)(2,1)S(1)} %collective-permute-done.8), channel_id=1, source_target_pairs={{0,1},{1,2},{2,3},{3,0},{4,5},{5,6},{6,7},{7,4},{8,9},{9,10},{10,1... | collective-permute-start | bytes 2752520 | tf_op jit(solution)/shard_map/ppermute | solution.py:80
  228.8 98.3 %collective-permute-start.17 = (bf16[896,512]{1,0:T(8,128)(2,1)S(1)}, bf16[896,512]{1,0:T(8,128)(2,1)S(1)}, u32[]{:S(2)}, u32[]{:S(2)}) collective-permute-start(bf16[896,512]{1,0:T(8,128)(2,1)S(1)} %collective-permute-done.9), channel_id=1, source_target_pairs={{0,1},{1,2},{2,3},{3,0},{4,5},{5,6},{6,7},{7,4},{8,9},{9,10},{10,1... | collective-permute-start | bytes 2752520 | tf_op jit(solution)/shard_map/ppermute | solution.py:80
  248.4 98.3 %collective-permute-start.18 = (bf16[896,512]{1,0:T(8,128)(2,1)S(1)}, bf16[896,512]{1,0:T(8,128)(2,1)S(1)}, u32[]{:S(2)}, u32[]{:S(2)}) collective-permute-start(bf16[896,512]{1,0:T(8,128)(2,1)S(1)} %collective-permute-done.10), channel_id=1, source_target_pairs={{0,1},{1,2},{2,3},{3,0},{4,5},{5,6},{6,7},{7,4},{8,9},{9,10},{10,1... | collective-permute-start | bytes 2752520 | tf_op jit(solution)/shard_map/ppermute | solution.py:80
  268.1 98.3 %collective-permute-start.19 = (bf16[896,512]{1,0:T(8,128)(2,1)S(1)}, bf16[896,512]{1,0:T(8,128)(2,1)S(1)}, u32[]{:S(2)}, u32[]{:S(2)}) collective-permute-start(bf16[896,512]{1,0:T(8,128)(2,1)S(1)} %collective-permute-done.11), channel_id=1, source_target_pairs={{0,1},{1,2},{2,3},{3,0},{4,5},{5,6},{6,7},{7,4},{8,9},{9,10},{10,1... | collective-permute-start | bytes 2752520 | tf_op jit(solution)/shard_map/ppermute | solution.py:80
  287.8 98.3 %collective-permute-start.22 = (bf16[896,512]{1,0:T(8,128)(2,1)S(1)}, bf16[896,512]{1,0:T(8,128)(2,1)S(1)}, u32[]{:S(2)}, u32[]{:S(2)}) collective-permute-start(bf16[896,512]{1,0:T(8,128)(2,1)S(1)} %collective-permute-done.14), channel_id=1, source_target_pairs={{0,1},{1,2},{2,3},{3,0},{4,5},{5,6},{6,7},{7,4},{8,9},{9,10},{10,1... | collective-permute-start | bytes 2752520 | tf_op jit(solution)/shard_map/ppermute | solution.py:80
  307.4 98.3 %collective-permute-start.21 = (bf16[896,512]{1,0:T(8,128)(2,1)S(1)}, bf16[896,512]{1,0:T(8,128)(2,1)S(1)}, u32[]{:S(2)}, u32[]{:S(2)}) collective-permute-start(bf16[896,512]{1,0:T(8,128)(2,1)S(1)} %collective-permute-done.13), channel_id=1, source_target_pairs={{0,1},{1,2},{2,3},{3,0},{4,5},{5,6},{6,7},{7,4},{8,9},{9,10},{10,1... | collective-permute-start | bytes 2752520 | tf_op jit(solution)/shard_map/ppermute | solution.py:80
  327.1 98.3 %collective-permute-start.20 = (bf16[896,512]{1,0:T(8,128)(2,1)S(1)}, bf16[896,512]{1,0:T(8,128)(2,1)S(1)}, u32[]{:S(2)}, u32[]{:S(2)}) collective-permute-start(bf16[896,512]{1,0:T(8,128)(2,1)S(1)} %collective-permute-done.12), channel_id=1, source_target_pairs={{0,1},{1,2},{2,3},{3,0},{4,5},{5,6},{6,7},{7,4},{8,9},{9,10},{10,1... | collective-permute-start | bytes 2752520 | tf_op jit(solution)/shard_map/ppermute | solution.py:80
  346.8 98.3 %collective-permute-start.23 = (bf16[896,512]{1,0:T(8,128)(2,1)S(1)}, bf16[896,512]{1,0:T(8,128)(2,1)S(1)}, u32[]{:S(2)}, u32[]{:S(2)}) collective-permute-start(bf16[896,512]{1,0:T(8,128)(2,1)S(1)} %collective-permute-done.15), channel_id=1, source_target_pairs={{0,1},{1,2},{2,3},{3,0},{4,5},{5,6},{6,7},{7,4},{8,9},{9,10},{10,1... | collective-permute-start | bytes 2752520 | tf_op jit(solution)/shard_map/ppermute | solution.py:80
  366.4 138.3 %collective-permute-start.24 = (bf16[896,512]{1,0:T(8,128)(2,1)S(1)}, bf16[896,512]{1,0:T(8,128)(2,1)S(1)}, u32[]{:S(2)}, u32[]{:S(2)}) collective-permute-start(bf16[896,512]{1,0:T(8,128)(2,1)S(1)} %collective-permute-done.16), channel_id=1, source_target_pairs={{0,1},{1,2},{2,3},{3,0},{4,5},{5,6},{6,7},{7,4},{8,9},{9,10},{10,1... | collective-permute-start | bytes 2752520 | tf_op jit(solution)/shard_map/ppermute | solution.py:80
  386.1 118.3 %collective-permute-start.25 = (bf16[896,512]{1,0:T(8,128)(2,1)S(1)}, bf16[896,512]{1,0:T(8,128)(2,1)S(1)}, u32[]{:S(2)}, u32[]{:S(2)}) collective-permute-start(bf16[896,512]{1,0:T(8,128)(2,1)S(1)} %collective-permute-done.17), channel_id=1, source_target_pairs={{0,1},{1,2},{2,3},{3,0},{4,5},{5,6},{6,7},{7,4},{8,9},{9,10},{10,1... | collective-permute-start | bytes 2752520 | tf_op jit(solution)/shard_map/ppermute | solution.py:80
  405.7 98.3 %collective-permute-start.26 = (bf16[896,512]{1,0:T(8,128)(2,1)S(1)}, bf16[896,512]{1,0:T(8,128)(2,1)S(1)}, u32[]{:S(2)}, u32[]{:S(2)}) collective-permute-start(bf16[896,512]{1,0:T(8,128)(2,1)S(1)} %collective-permute-done.18), channel_id=1, source_target_pairs={{0,1},{1,2},{2,3},{3,0},{4,5},{5,6},{6,7},{7,4},{8,9},{9,10},{10,1... | collective-permute-start | bytes 2752520 | tf_op jit(solution)/shard_map/ppermute | solution.py:80
  425.4 94.1 %collective-permute-start.27 = (bf16[896,512]{1,0:T(8,128)(2,1)S(1)}, bf16[896,512]{1,0:T(8,128)(2,1)S(1)}, u32[]{:S(2)}, u32[]{:S(2)}) collective-permute-start(bf16[896,512]{1,0:T(8,128)(2,1)S(1)} %collective-permute-done.19), channel_id=1, source_target_pairs={{0,1},{1,2},{2,3},{3,0},{4,5},{5,6},{6,7},{7,4},{8,9},{9,10},{10,1... | collective-permute-start | bytes 2752520 | tf_op jit(solution)/shard_map/ppermute | solution.py:80
  519.8 4.0 copy-start.1
